TPU v7x, 256 devices: a whole 4x4x8 slice. The times are simulated.
256 devices in a mesh: seq: 32 (over x, z_hi, core), ch: 8 (over z_lo, y).
Axes of the slice: x: 4, y: 4, z: 8 (z_hi: 4, z_lo: 2; z = z_hi * 2 + z_lo), core: 2. Of those that a mesh axis runs over, the one named last changes fastest.
Arguments:
- queries: bfloat16 [8192, 4096], P('seq', 'ch'), may hold values from -6 to 6
- key_in: bfloat16 [8192, 4096], P('seq', 'ch'), may hold values from -6 to 6
- value_in: bfloat16 [8192, 4096], P('seq', 'ch'), may hold values from -6 to 6
- filter_raw: bfloat16 [8192, 4096], P('seq', 'ch'), may hold values from -6 to 6
- skip_gain: float32 [4096], P('ch'), may hold values from -4 to 4
- out_weight: bfloat16 [4096, 4096], P('ch'), may hold values from -0.09375 to 0.09375
- cotangent: bfloat16 [8192, 4096], P('seq', 'ch'), may hold values from -6 to 6
Outputs:
- projected: bfloat16 [8192, 4096], P('seq', 'ch')
- grad_query: bfloat16 [8192, 4096], P('seq', 'ch')
- grad_key: bfloat16 [8192, 4096], P('seq', 'ch')
- grad_value: bfloat16 [8192, 4096], P('seq', 'ch')
- grad_filter: bfloat16 [8192, 4096], P('seq', 'ch')
All inputs are finite; a program needn't handle non-finite values.
Results may differ from a plain program's by a relative error of at most 0.015.
Values may be sent and summed in bfloat16 or wider, within the bound.
No kernel may reach another device: no remote copies, remote signals or barrier semaphores. Data moves between devices by JAX's collectives and lax.ppermute only.
A program may use at most 128 MiB of HBM per device.

v0:
```python
import math

import jax
import jax.numpy as jnp
from jax import lax
from jax.sharding import PartitionSpec as P

precise = lax.Precision.HIGHEST


def in_order(blocks, dim):
    dims = list(blocks.shape[1:])
    dims[dim] *= blocks.shape[0]
    return jnp.moveaxis(blocks, 0, dim).reshape(dims)


def from_everyone(value, axis):
    copies = jnp.broadcast_to(value, (lax.axis_size(axis), *value.shape))
    return lax.all_to_all(copies, axis, split_axis=0, concat_axis=0, tiled=True)


def gathered_copies(value, axis, dim):
    return in_order(from_everyone(value, axis), dim)


def in_blocks(value, dim, peers):
    before, after = (value.shape[:dim], value.shape[dim + 1 :])
    return jnp.moveaxis(value.reshape(*before, peers, -1, *after), dim, 0)


def sent_and_summed(value, axis, dim):
    peers = lax.axis_size(axis)
    blocks = lax.all_to_all(in_blocks(value, dim, peers), axis, 0, 0, tiled=True)
    return jnp.sum(blocks.astype(jnp.float32), axis=0)


def phase_table(height, breadth, period, row_start, column_start):
    row_index = (row_start + lax.iota(jnp.int32, height))[:, None]
    column_index = (column_start + lax.iota(jnp.int32, breadth))[None, :]
    residue = row_index * column_index % period
    angles = residue.astype(jnp.float32) * (2.0 * math.pi / period)
    return (jnp.cos(angles), jnp.sin(angles))


def over_blocks(pieces, total_blocks):
    cosine_table, sine_table = phase_table(total_blocks, pieces.shape[1], total_blocks, 0, 0)
    values = pieces.astype(jnp.float32)
    real_part = jnp.einsum("kj,sj...->sk...", cosine_table, values, precision=precise)
    imag_part = -jnp.einsum("kj,sj...->sk...", sine_table, values, precision=precise)
    return (real_part, imag_part)


def under_blocks(real_part, imag_part, kept_blocks):
    cosine_table, sine_table = phase_table(
        kept_blocks, real_part.shape[1], real_part.shape[1], 0, 0
    )
    first_term = jnp.einsum("jk,sk...->sj...", cosine_table, real_part, precision=precise)
    second_term = jnp.einsum("jk,sk...->sj...", sine_table, imag_part, precision=precise)
    return first_term - second_term


def rotate(real_part, imag_part, freq_start, row_start, period, direction):
    row_count = real_part.shape[3]
    cosine_table, sine_table = phase_table(
        real_part.shape[1], row_count, period, freq_start, row_start
    )
    cosine_table = cosine_table[None, :, None, :]
    sine_table = direction * sine_table[None, :, None, :]
    return (
        real_part * cosine_table - imag_part * sine_table,
        real_part * sine_table + imag_part * cosine_table,
    )


def over_rows(real_part, imag_part, direction):
    length_rows = real_part.shape[3]
    cosine_table, sine_table = phase_table(length_rows, length_rows, length_rows, 0, 0)
    sine_table = direction * sine_table
    form = "mr,skcr->skcm"

    def contract(table, values):
        return jnp.einsum(form, table, values, precision=precise)

    new_real = contract(cosine_table, real_part) - contract(sine_table, imag_part)
    new_imag = contract(cosine_table, imag_part) + contract(sine_table, real_part)
    return (new_real, new_imag)


def transform(signals):
    seq_devices = lax.axis_size("seq")
    local_rows = signals.shape[1]
    total_blocks = 2 * seq_devices
    period = total_blocks * local_rows
    flipped = jnp.transpose(signals, (0, 2, 1))[:, None]
    pieces = lax.all_to_all(flipped, "seq", split_axis=2, concat_axis=1, tiled=True)
    real_part, imag_part = over_blocks(pieces, total_blocks)
    real_part, imag_part = rotate(real_part, imag_part, 0, 0, period, -1.0)
    return over_rows(real_part, imag_part, -1.0)


def inverse(real_part, imag_part):
    seq_devices = lax.axis_size("seq")
    local_rows = real_part.shape[3]
    period = 2 * seq_devices * local_rows
    real_part, imag_part = over_rows(real_part, imag_part, 1.0)
    real_part, imag_part = rotate(real_part, imag_part, 0, 0, period, 1.0)
    values = under_blocks(real_part, imag_part, seq_devices)
    values = lax.all_to_all(
        values.astype(jnp.bfloat16), "seq", split_axis=1, concat_axis=2, tiled=True
    ).astype(values.dtype)
    return jnp.transpose(values[:, 0], (0, 2, 1))


def on_device(queries, key_in, value_in, filter_raw, skip_gain, out_weight, cotangent):
    local_rows, local_width = queries.shape
    seq_devices = lax.axis_size("seq")
    full_length = local_rows * seq_devices
    factor = 1.0 / (math.sqrt(full_length) * 2.0 * full_length)
    grad_mixed = lax.dot_general(
        gathered_copies(cotangent, "ch", 1),
        out_weight,
        (((1,), (1,)), ((), ())),
        preferred_element_type=jnp.float32,
    )
    product_kv = (key_in.astype(jnp.float32) * value_in.astype(jnp.float32)).astype(jnp.bfloat16)
    grad_conv = (grad_mixed * queries.astype(jnp.float32)).astype(jnp.bfloat16)
    real_part, imag_part = transform(jnp.stack([product_kv, filter_raw, grad_conv]))
    z_real, h_real, g_real = (real_part[0], real_part[1], real_part[2])
    z_imag, h_imag, g_imag = (imag_part[0], imag_part[1], imag_part[2])
    conv_real = h_real * z_real - h_imag * z_imag
    conv_imag = h_real * z_imag + h_imag * z_real
    back_real = h_real * g_real + h_imag * g_imag
    back_imag = h_real * g_imag - h_imag * g_real
    taps_real = z_real * g_real + z_imag * g_imag
    taps_imag = z_real * g_imag - z_imag * g_real
    results = inverse(
        jnp.stack([conv_real, back_real, taps_real]), jnp.stack([conv_imag, back_imag, taps_imag])
    )
    results = results * factor
    convolved = results[0] + skip_gain * product_kv.astype(jnp.float32)
    gated_output = (queries.astype(jnp.float32) * convolved).astype(jnp.bfloat16)
    partial_terms = jnp.dot(gated_output, out_weight, preferred_element_type=jnp.float32)
    projected = sent_and_summed(partial_terms.astype(jnp.bfloat16), "ch", 1).astype(jnp.bfloat16)
    grad_query = (grad_mixed * convolved).astype(jnp.bfloat16)
    grad_product = results[1] + skip_gain * grad_conv.astype(jnp.float32)
    grad_key = (grad_product * value_in.astype(jnp.float32)).astype(jnp.bfloat16)
    grad_value = (grad_product * key_in.astype(jnp.float32)).astype(jnp.bfloat16)
    grad_filter = results[2].astype(jnp.bfloat16)
    return (projected, grad_query, grad_key, grad_value, grad_filter)


def solution(mesh):
    placed = (
        P("seq", "ch"),
        P("seq", "ch"),
        P("seq", "ch"),
        P("seq", "ch"),
        P("ch"),
        P("ch", None),
        P("seq", "ch"),
    )
    return jax.shard_map(
        on_device,
        mesh=mesh,
        in_specs=placed,
        out_specs=(P("seq", "ch"), P("seq", "ch"), P("seq", "ch"), P("seq", "ch"), P("seq", "ch")),
        check_vma=False,
    )
```

profile of v0, /device:TPU:1, one launch (start us, length us, event | category | flops | bytes accessed | tf_op | source)
XLA Modules:
  0.0 203.7 jit_solution(3127725182108790286)
XLA Ops:
  0.6 1.1 copy.37
  1.7 0.0 copy-start.1
  1.7 0.0 copy-start.2
  1.7 0.0 copy-start.7
  1.8 1.5 broadcast_in_dim.4
  3.2 6.4 %all-to-all-start = ((bf16[8,256,512]{1,2,0:T(8,128)(2,1)}), bf16[8,256,512]{1,2,0:T(8,128)(2,1)S(1)}, u32[]{:S(2)}, u32[]{:S(2)}) async-start(bf16[8,256,512]{1,2,0:T(8,128)(2,1)} %broadcast_in_dim.4), calls=%async_computation | async-start | bytes 4194304 | tf_op jit(solution)/shard_map/all_to_all | solution.py:19
  9.6 0.0 copy-done.1
  9.6 0.0 copy-done.2
  9.6 0.1 fusion.172
  9.7 26.1 %all-to-all-done = bf16[8,256,512]{1,2,0:T(8,128)(2,1)S(1)} async-done(((bf16[8,256,512]{1,2,0:T(8,128)(2,1)}), bf16[8,256,512]{1,2,0:T(8,128)(2,1)S(1)}, u32[]{:S(2)}, u32[]{:S(2)}) %all-to-all-start) | async-done | bytes 2097184 | tf_op jit(solution)/shard_map/all_to_all | solution.py:19
  35.8 4.3 %fusion.51 = (bf16[256,512]{1,0:T(8,128)(2,1)S(1)}, f32[256,512]{1,0:T(8,128)}) fusion(bf16[256,512]{1,0:T(8,128)(2,1)S(1)} %copy-done.7, bf16[256,4096]{0,1:T(8,128)(2,1)S(1)} %bitcast.114, bf16[512,4096]{1,0:T(8,128)(2,1)} %param.12), kind=kOutput, calls=%fused_computation.61 | convolution fusion | flops 1074135040 | bytes 7340032 | tf_op jit(solution)/shard_map/dot_general | solution.py:119
  40.1 0.7 copy-done.4
  40.8 0.0 copy-done.8
  40.8 0.1 maximum_bitcast_fusion
  40.9 1.4 copy.38
  42.3 11.2 %all-to-all-start.1 = ((bf16[3,1,512,256]{3,0,1,2:T(4,128)(2,1)}), bf16[3,1,512,256]{3,0,1,2:T(4,128)(2,1)S(1)}, u32[]{:S(2)}, u32[]{:S(2)}) async-start(bf16[3,1,512,256]{3,0,1,2:T(4,128)(2,1)} %copy.38), calls=%async_computation.1 | async-start | bytes 2097152 | tf_op jit(solution)/shard_map/all_to_all | solution.py:95
  53.5 0.3 fusion.95
  53.8 0.3 broadcast_multiply_fusion
  54.1 24.2 %all-to-all-done.1 = bf16[3,1,512,256]{3,0,1,2:T(4,128)(2,1)S(1)} async-done(((bf16[3,1,512,256]{3,0,1,2:T(4,128)(2,1)}), bf16[3,1,512,256]{3,0,1,2:T(4,128)(2,1)S(1)}, u32[]{:S(2)}, u32[]{:S(2)}) %all-to-all-start.1) | async-done | bytes 786464 | tf_op jit(solution)/shard_map/all_to_all | solution.py:95
  78.2 0.1 copy.39
  78.4 1.5 fusion.47
  79.9 2.2 %fusion = (f32[3,64,16,256]{3,1,2,0:T(8,128)S(1)}, f32[3,64,16,256]{3,1,2,0:T(8,128)S(1)}) fusion(f32[3,16,256,64]{2,3,1,0:T(8,128)S(1)} %fusion.47, f32[64,256]{1,0:T(8,128)S(1)} %get-tuple-element.18, f32[64,256]{1,0:T(8,128)S(1)} %get-tuple-element.19, bf16[3,32,16,256]{3,2,1,0:T(8,128)(2,1)S(1)} %bitcast.112), kind=kOutput, calls=%fused_computation.5 | convolution fusion | flops 307523584 | bytes 10354688 | tf_op jit(solution)/shard_map/kj,sj...->sk.../dot_general | solution.py:48
  82.1 5.2 %fusion.20 = f32[3,64,16,256]{3,2,1,0:T(8,128)S(1)} fusion(f32[3,64,16,256]{3,1,2,0:T(8,128)S(1)} %get-tuple-element.6), kind=kOutput, calls=%fused_computation.27 | convolution fusion | flops 2416902144 | bytes 6291456 | tf_op jit(solution)/shard_map/mr,skcr->skcm/dot_general | solution.py:82
  87.3 5.8 %fusion.18 = f32[3,64,16,256]{3,2,1,0:T(8,128)S(1)} fusion(f32[3,64,16,256]{3,1,2,0:T(8,128)S(1)} %get-tuple-element.6), kind=kOutput, calls=%fused_computation.25 | convolution fusion | flops 2416836608 | bytes 6291456 | tf_op jit(solution)/shard_map/mr,skcr->skcm/dot_general | solution.py:82
  93.2 5.2 %fusion.26 = f32[3,64,16,256]{3,2,1,0:T(8,128)S(1)} fusion(f32[3,64,16,256]{3,2,1,0:T(8,128)S(1)} %fusion.20, f32[3,64,16,256]{3,1,2,0:T(8,128)S(1)} %get-tuple-element.5), kind=kOutput, calls=%fused_computation.34 | convolution fusion | flops 2417623040 | bytes 9437184 | tf_op jit(solution)/shard_map/mr,skcr->skcm/dot_general | solution.py:82
  98.4 5.5 %fusion.29 = f32[3,64,16,256]{3,2,1,0:T(8,128)S(1)} fusion(f32[3,64,16,256]{3,2,1,0:T(8,128)S(1)} %fusion.18, f32[3,64,16,256]{3,1,2,0:T(8,128)S(1)} %get-tuple-element.5), kind=kOutput, calls=%fused_computation.35 | convolution fusion | flops 2417688576 | bytes 9437184 | tf_op jit(solution)/shard_map/mr,skcr->skcm/dot_general | solution.py:82
  103.9 0.9 multiply_subtract_fusion.2
  104.8 0.8 multiply_add_fusion.2
  105.6 0.3 pad_maximum_fusion.1
  105.9 5.1 %fusion.12 = f32[3,64,16,256]{3,1,2,0:T(8,128)S(1)} fusion(f32[3,64,16,256]{3,2,1,0:T(8,128)S(1)} %pad_maximum_fusion.1), kind=kOutput, calls=%fused_computation.19 | convolution fusion | flops 2416836608 | bytes 6291456 | tf_op jit(solution)/shard_map/mr,skcr->skcm/dot_general | solution.py:82
  111.0 5.7 %fusion.10 = f32[3,64,16,256]{3,1,2,0:T(8,128)S(1)} fusion(f32[3,64,16,256]{3,2,1,0:T(8,128)S(1)} %pad_maximum_fusion.1), kind=kOutput, calls=%fused_computation.17 | convolution fusion | flops 2416836608 | bytes 6291456 | tf_op jit(solution)/shard_map/mr,skcr->skcm/dot_general | solution.py:82
  116.7 0.3 pad_maximum_fusion
  117.0 5.1 %fusion.32 = f32[3,64,16,256]{3,1,2,0:T(8,128)S(1)} fusion(f32[3,64,16,256]{3,1,2,0:T(8,128)S(1)} %fusion.12, f32[3,64,16,256]{3,2,1,0:T(8,128)S(1)} %pad_maximum_fusion), kind=kOutput, calls=%fused_computation.36 | convolution fusion | flops 2417623040 | bytes 9437184 | tf_op jit(solution)/shard_map/mr,skcr->skcm/dot_general | solution.py:82
  122.2 5.6 %fusion.35 = f32[3,64,16,256]{3,1,2,0:T(8,128)S(1)} fusion(f32[3,64,16,256]{3,1,2,0:T(8,128)S(1)} %fusion.10, f32[3,64,16,256]{3,2,1,0:T(8,128)S(1)} %pad_maximum_fusion), kind=kOutput, calls=%fused_computation.37 | convolution fusion | flops 2417623040 | bytes 9437184 | tf_op jit(solution)/shard_map/mr,skcr->skcm/dot_general | solution.py:82
  127.8 2.3 %fusion.2 = f32[3,16,256,32]{2,3,1,0:T(8,128)S(1)} fusion(f32[3,64,16,256]{3,1,2,0:T(8,128)S(1)} %fusion.35, f32[3,64,16,256]{3,1,2,0:T(8,128)S(1)} %fusion.32, f32[64,256]{1,0:T(8,128)S(1)} %fusion.95, f32[64,256]{1,0:T(8,128)S(1)} %get-tuple-element.19), kind=kOutput, calls=%fused_computation.9 | convolution fusion | flops 304377856 | bytes 7995392 | tf_op jit(solution)/shard_map/jk,sk...->sj.../dot_general | solution.py:58
  130.1 2.5 %fusion.44 = bf16[3,32,16,256]{3,1,2,0:T(8,128)(2,1)S(1)} fusion(f32[3,16,256,32]{2,3,1,0:T(8,128)S(1)} %fusion.2, f32[3,64,16,256]{3,1,2,0:T(8,128)S(1)} %fusion.35, f32[3,64,16,256]{3,1,2,0:T(8,128)S(1)} %fusion.32, f32[64,256]{1,0:T(8,128)S(1)} %fusion.95, f32[64,256]{1,0:T(8,128)S(1)} %get-tuple-element.19), kind=kOutput, calls=%fused_computation.44 | convolution fusion | flops 305164288 | bytes 8781824 | tf_op jit(solution)/shard_map/jk,sk...->sj.../dot_general | solution.py:57
  132.6 0.4 copy.50
  133.1 29.1 %all_to_all.31 = bf16[3,32,16,256]{3,2,0,1:T(8,128)(2,1)S(1)} all-to-all(bf16[3,32,16,256]{3,2,0,1:T(8,128)(2,1)S(1)} %copy.50), channel_id=1, replica_groups=mesh['seq'=32,'ch'=8] {'seq'}, dimensions={1} | all-to-all | bytes 1572864 | tf_op jit(solution)/shard_map/all_to_all | solution.py:108
  162.1 0.2 convert_multiply_fusion
  162.4 0.5 copy.52
  162.9 4.2 %convolution_convert_fusion = bf16[256,4096]{1,0:T(8,128)(2,1)S(1)} fusion(bf16[512,4096]{1,0:T(8,128)(2,1)} %param.12, bf16[256,512]{1,0:T(8,128)(2,1)} %param.7, f32[3,256,512]{2,1,0:T(8,128)S(1)} %bitcast.108, f32[512]{0:T(512)S(1)} %copy-done.9, bf16[256,512]{1,0:T(8,128)(2,1)S(1)} %copy-done.1, bf16[256,512]{1,0:T(8,128)(2,1)} %param.8), kind=kOutput, calls=%fused_computation | convolution fusion | flops 1076101120 | bytes 7604224 | tf_op jit(solution)/shard_map/dot_general | solution.py:142
  167.1 1.5 copy.100
  168.6 7.4 %all-to-all-start.3 = ((bf16[8,256,512]{2,1,0:T(8,128)(2,1)}), bf16[8,256,512]{2,1,0:T(8,128)(2,1)S(1)}, u32[]{:S(2)}, u32[]{:S(2)}) async-start(bf16[8,256,512]{2,1,0:T(8,128)(2,1)} %bitcast.106), calls=%async_computation.3 | async-start | bytes 4194304 | tf_op jit(solution)/shard_map/all_to_all | solution.py:33
  176.0 1.8 fusion.61
  177.8 0.0 copy-done.6
  177.8 2.3 %fusion.53 = (bf16[256,512]{1,0:T(8,128)(2,1)}, bf16[256,512]{1,0:T(8,128)(2,1)}, bf16[256,512]{1,0:T(8,128)(2,1)}) fusion(bf16[256,512]{1,0:T(8,128)(2,1)S(1)} %copy-done.3, bf16[256,512]{1,0:T(8,128)(2,1)S(1)} %copy-done.5, f32[3,256,512]{2,1,0:T(8,128)} %bitcast.110, f32[512]{0:T(512)S(1)} %copy-done.9, bf16[256,512]{1,0:T(8,128)(2,1)S(1)} %copy-done.1, ...), kind=kLoop, calls=%fused_computation.63 | loop fusion | flops 2097152 | bytes 3147776 | tf_op jit(solution)/shard_map/convert_element_type | solution.py:147
  180.1 22.1 %all-to-all-done.3 = bf16[8,256,512]{2,1,0:T(8,128)(2,1)S(1)} async-done(((bf16[8,256,512]{2,1,0:T(8,128)(2,1)}), bf16[8,256,512]{2,1,0:T(8,128)(2,1)S(1)}, u32[]{:S(2)}, u32[]{:S(2)}) %all-to-all-start.3) | async-done | bytes 2097184 | tf_op jit(solution)/shard_map/all_to_all | solution.py:33
  202.2 1.0 reduce_sum.12
  (12 shorter events, 0.0 us)
Async XLA Ops:
  1.7 7.9 %copy-start.1 = (bf16[256,512]{1,0:T(8,128)(2,1)S(1)}, bf16[256,512]{1,0:T(8,128)(2,1)}, u32[]{:S(2)}) copy-start(bf16[256,512]{1,0:T(8,128)(2,1)} %param.9) | copy-start | bytes 786436
  1.7 7.9 %copy-start.2 = (bf16[256,512]{1,0:T(8,128)(2,1)S(1)}, bf16[256,512]{1,0:T(8,128)(2,1)}, u32[]{:S(2)}) copy-start(bf16[256,512]{1,0:T(8,128)(2,1)} %param.8) | copy-start | bytes 786436
  1.7 34.1 %copy-start.7 = (bf16[256,512]{1,0:T(8,128)(2,1)S(1)}, bf16[256,512]{1,0:T(8,128)(2,1)}, u32[]{:S(2)}) copy-start(bf16[256,512]{1,0:T(8,128)(2,1)} %param.7) | copy-start | bytes 786436
  3.2 32.6 %all-to-all-start = ((bf16[8,256,512]{1,2,0:T(8,128)(2,1)}), bf16[8,256,512]{1,2,0:T(8,128)(2,1)S(1)}, u32[]{:S(2)}, u32[]{:S(2)}) async-start(bf16[8,256,512]{1,2,0:T(8,128)(2,1)} %broadcast_in_dim.4), calls=%async_computation | async-start | bytes 4194304 | tf_op jit(solution)/shard_map/all_to_all | solution.py:19
  35.8 5.0 %copy-start.8 = (bf16[256,512]{1,0:T(8,128)(2,1)S(1)}, bf16[256,512]{1,0:T(8,128)(2,1)}, u32[]{:S(2)}) copy-start(bf16[256,512]{1,0:T(8,128)(2,1)} %param.10) | copy-start | bytes 786436
  40.1 0.7 copy-start.4
  42.3 35.9 %all-to-all-start.1 = ((bf16[3,1,512,256]{3,0,1,2:T(4,128)(2,1)}), bf16[3,1,512,256]{3,0,1,2:T(4,128)(2,1)S(1)}, u32[]{:S(2)}, u32[]{:S(2)}) async-start(bf16[3,1,512,256]{3,0,1,2:T(4,128)(2,1)} %copy.38), calls=%async_computation.1 | async-start | bytes 2097152 | tf_op jit(solution)/shard_map/all_to_all | solution.py:95
  162.1 0.7 copy-start.9
  162.8 4.2 %copy-start = (f32[3,512,256]{1,2,0:T(8,128)}, f32[3,512,256]{1,2,0:T(8,128)S(1)}, u32[]{:S(2)}) copy-start(f32[3,512,256]{1,2,0:T(8,128)S(1)} %copy.52) | copy-start | bytes 4718596
  168.6 9.2 %copy-start.3 = (bf16[256,512]{1,0:T(8,128)(2,1)S(1)}, bf16[256,512]{1,0:T(8,128)(2,1)}, u32[]{:S(2)}) copy-start(bf16[256,512]{1,0:T(8,128)(2,1)} %param.8) | copy-start | bytes 786436
  168.6 9.2 %copy-start.5 = (bf16[256,512]{1,0:T(8,128)(2,1)S(1)}, bf16[256,512]{1,0:T(8,128)(2,1)}, u32[]{:S(2)}) copy-start(bf16[256,512]{1,0:T(8,128)(2,1)} %copy-done.4) | copy-start | bytes 786436
  168.6 9.2 %copy-start.6 = (f32[256,512]{1,0:T(8,128)S(1)}, f32[256,512]{1,0:T(8,128)}, u32[]{:S(2)}) copy-start(f32[256,512]{1,0:T(8,128)} %get-tuple-element.17) | copy-start | bytes 1572868
  168.6 33.6 %all-to-all-start.3 = ((bf16[8,256,512]{2,1,0:T(8,128)(2,1)}), bf16[8,256,512]{2,1,0:T(8,128)(2,1)S(1)}, u32[]{:S(2)}, u32[]{:S(2)}) async-start(bf16[8,256,512]{2,1,0:T(8,128)(2,1)} %bitcast.106), calls=%async_computation.3 | async-start | bytes 4194304 | tf_op jit(solution)/shard_map/all_to_all | solution.py:33
where the time goes:
time: 207 us; the launch traced here: 204 us
  waiting for transfers between devices  72.4 us (35%)
  matrix products  60.3 us (29%)
  blocking collectives  29.1 us (14%)
  starting transfers between devices  24.9 us (12%)
  local copies, waits for them, and re-layouts  9.02 us (4%)
  other arithmetic  6.53 us (3%)
    dot_general x8, matrix products, contract(): return jnp.einsum(form, table, values, precision=precise)  43.3 us
    all_to_all x1, blocking collectives, inverse(): lax.all_to_all(values.astype(jnp.bfloat16), 'seq', split_axis=1, concat_a...  29.1 us
    all_to_all x1, waiting for transfers between devices, from_everyone(): return lax.all_to_all(copies, axis, split_axis=0, concat_axis=0, tiled=True)  26.1 us
    all_to_all x1, waiting for transfers between devices, transform(): lax.all_to_all(flipped, 'seq', split_axis=2, concat_axis=1, tiled=True)  24.2 us
    all_to_all x1, waiting for transfers between devices, sent_and_summed(): lax.all_to_all(in_blocks(value, dim, peers), axis, 0, 0, tiled=True)  22.1 us
    all_to_all x1, starting transfers between devices, transform(): lax.all_to_all(flipped, 'seq', split_axis=2, concat_axis=1, tiled=True)  11.2 us
    all_to_all x1, starting transfers between devices, sent_and_summed(): lax.all_to_all(in_blocks(value, dim, peers), axis, 0, 0, tiled=True)  7.4 us
    all_to_all x1, starting transfers between devices, from_everyone(): return lax.all_to_all(copies, axis, split_axis=0, concat_axis=0, tiled=True)  6.36 us
  transfers between devices with their start and end apart: 3, of which 3 were waited for; matrix products, arithmetic and copies ran while one was open for 2% of the time, Pallas kernels for 0%

commit v1 on v0

v1 whole, which is shorter than its diff:
```python
import math

import jax
import jax.numpy as jnp
import numpy as np
from jax import lax
from jax.experimental import pallas as pl
from jax.experimental.pallas import tpu as pltpu
from jax.sharding import PartitionSpec as P

bf16 = jnp.bfloat16
f32 = jnp.float32
LANES = 128


def split(table):
    high = table.astype(bf16)
    low = (table - high.astype(np.float64)).astype(bf16)
    return np.asarray(high), np.asarray(low)


def tables(length, devices):
    points = 2 * length
    half = points // LANES // 2
    parts = half // devices
    rows = np.arange(half)
    j = parts * (rows % devices) + rows // devices
    k1 = np.arange(half) + 0.5
    lanes = np.arange(LANES)
    angle = 2.0 * np.pi / (2 * half) * np.outer(k1, j)
    first = np.concatenate([np.cos(angle), -np.sin(angle)], 0)
    last = np.concatenate([np.cos(angle.T), -np.sin(angle.T)], 1)
    turn = 2.0 * np.pi / points * np.outer(k1, lanes)
    factor = 2.0 / (points * math.sqrt(length))
    turns = np.stack([np.cos(turn), -np.sin(turn), np.cos(turn) * factor, np.sin(turn) * factor])
    phase = 2.0 * np.pi / LANES * (np.outer(lanes, lanes) % LANES)
    c, s = np.cos(phase), np.sin(phase)
    over = np.block([[c, -s], [s, c]])
    under = np.block([[c, s], [-s, c]])
    first_high, first_low = split(first)
    last_high, last_low = split(last)
    return (
        np.concatenate([first_high, first_low], 0),
        np.stack(split(over)),
        np.stack(split(under)),
        np.concatenate([last_high, last_low], 0),
        turns.astype(np.float32),
    )


def dot(a, b):
    return lax.dot_general(a, b, (((1,), (0,)), ((), ())), preferred_element_type=f32)


def halves(x):
    high = x.astype(bf16)
    return high, (x - high.astype(f32)).astype(bf16)


def forward(x, first, turns):
    half = turns.shape[1]
    both = dot(first, x)
    a = both[: 2 * half] + both[2 * half :]
    real, imag = a[:half], a[half:]
    return jnp.concatenate(
        [real * turns[0] - imag * turns[1], real * turns[1] + imag * turns[0]], 1
    )


def lanes_dot(x, table):
    high, low = halves(x)
    return dot(high, table[0]) + dot(low, table[0]) + dot(high, table[1])


def backward(b, last, turns):
    half = turns.shape[1]
    real, imag = b[:, :LANES], b[:, LANES:]
    d = jnp.concatenate([real * turns[2] - imag * turns[3], real * turns[3] + imag * turns[2]], 0)
    high, low = halves(d)
    rows = last.shape[0] // 2
    both = dot(last, high)
    return both[:rows] + both[rows:] + dot(last[:rows], low)


def rows_of(x):
    parts = x.shape[-1] // LANES
    return jnp.concatenate([x[:, p * LANES : (p + 1) * LANES] for p in range(parts)], 0)


def unrows(y, devices):
    return jnp.concatenate(
        [y[p * devices : (p + 1) * devices] for p in range(y.shape[0] // devices)], 1
    )


def product(a, b, conjugate):
    ar, ai = a[:, :LANES], a[:, LANES:]
    br, bi = b[:, :LANES], b[:, LANES:]
    if conjugate:
        return jnp.concatenate([ar * br + ai * bi, ar * bi - ai * br], 1)
    return jnp.concatenate([ar * br - ai * bi, ar * bi + ai * br], 1)


def prepare_body(key_ref, value_ref, filter_ref, out_ref, pkv_ref):
    peers, _, width, local_rows = out_ref.shape
    pkv = (key_ref[...].astype(f32) * value_ref[...].astype(f32)).astype(bf16)
    pkv_ref[...] = pkv
    out_ref[:, 0] = pkv.T.reshape(peers, width, local_rows)
    out_ref[:, 1] = filter_ref[...].T.reshape(peers, width, local_rows)


def conv_body(x_ref, first_ref, over_ref, under_ref, last_ref, turns_ref, out_ref, spec_ref, a_ref):
    width, devices = x_ref.shape[1:3]
    half = turns_ref.shape[1]
    for s in range(2):
        for c in range(width):
            a_ref[s, c] = forward(rows_of(x_ref[s, c]), first_ref[...], turns_ref)
    spectra = lanes_dot(a_ref[...].reshape(2 * width * half, 2 * LANES), over_ref)
    spec_ref[...] = spectra.reshape(spec_ref.shape)
    for c in range(width):
        a_ref[0, c] = product(spec_ref[1, c], spec_ref[0, c], False)
    b = lanes_dot(a_ref[0].reshape(width * half, 2 * LANES), under_ref)
    a_ref[1] = b.reshape(width, half, 2 * LANES)
    for c in range(width):
        y = backward(a_ref[1, c], last_ref[...], turns_ref)
        out_ref[c] = unrows(y.astype(bf16), devices)


def back_body(x_ref, spec_ref, first_ref, over_ref, under_ref, last_ref, turns_ref, out_ref, a_ref):
    width, devices = x_ref.shape[:2]
    half = turns_ref.shape[1]
    for c in range(width):
        a_ref[0, c] = forward(rows_of(x_ref[c]), first_ref[...], turns_ref)
    g = lanes_dot(a_ref[0].reshape(width * half, 2 * LANES), over_ref)
    a_ref[0] = g.reshape(width, half, 2 * LANES)
    for c in range(width):
        g_c = a_ref[0, c]
        a_ref[1, c] = product(spec_ref[0, c], g_c, True)
        a_ref[0, c] = product(spec_ref[1, c], g_c, True)
    b = lanes_dot(a_ref[...].reshape(2 * width * half, 2 * LANES), under_ref)
    a_ref[...] = b.reshape(a_ref.shape)
    for s in range(2):
        for c in range(width):
            y = backward(a_ref[s, c], last_ref[...], turns_ref)
            out_ref[s, c] = unrows(y.astype(bf16), devices)


def mixed_body(cot_ref, weight_ref, queries_ref, mixed_ref, conv_ref, sent_ref):
    step = pl.program_id(0)
    term = lax.dot_general(
        cot_ref[0], weight_ref[...], (((1,), (1,)), ((), ())), preferred_element_type=f32
    )

    @pl.when(step == 0)
    def _():
        mixed_ref[...] = term

    @pl.when(step > 0)
    def _():
        mixed_ref[...] += term

    @pl.when(step == pl.num_programs(0) - 1)
    def _():
        g = (mixed_ref[...] * queries_ref[...].astype(f32)).astype(bf16)
        conv_ref[...] = g
        sent_ref[...] = g.T.reshape(sent_ref.shape)


def gate_body(conv_ref, pkv_ref, skip_ref, queries_ref, weight_ref, out_ref, convolved_ref, gated_ref):
    @pl.when(pl.program_id(0) == 0)
    def _():
        local_rows = queries_ref.shape[0]
        conv = conv_ref[...].reshape(-1, local_rows).T.astype(f32)
        convolved = conv + skip_ref[...] * pkv_ref[...].astype(f32)
        convolved_ref[...] = convolved
        gated_ref[...] = (queries_ref[...].astype(f32) * convolved).astype(bf16)

    out_ref[0] = dot(gated_ref[...], weight_ref[...]).astype(bf16)


def finish_body(res_ref, conv_ref, skip_ref, key_ref, value_ref, gk_ref, gv_ref, gf_ref):
    local_rows = key_ref.shape[0]
    gf_ref[...] = res_ref[:, 1].reshape(-1, local_rows).T
    product_grad = res_ref[:, 0].reshape(-1, local_rows).T.astype(f32)
    product_grad = product_grad + skip_ref[...] * conv_ref[...].astype(f32)
    gk_ref[...] = (product_grad * value_ref[...].astype(f32)).astype(bf16)
    gv_ref[...] = (product_grad * key_ref[...].astype(f32)).astype(bf16)


def cost(flops, nbytes):
    return pl.CostEstimate(flops=flops, transcendentals=0, bytes_accessed=nbytes)


def to_all(x, axis):
    return lax.all_to_all(x, axis, split_axis=0, concat_axis=0, tiled=True)


def on_device(queries, key_in, value_in, filter_raw, skip_gain, out_weight, cotangent):
    local_rows, local_width = queries.shape
    seq_devices = lax.axis_size("seq")
    ch_devices = lax.axis_size("ch")
    length = local_rows * seq_devices
    width = local_width // seq_devices
    half = length // LANES
    shape = jax.ShapeDtypeStruct
    table = [jnp.asarray(t) for t in tables(length, seq_devices)]
    skip = skip_gain.reshape(1, local_width)
    message = (seq_devices, width, local_rows)

    copies = to_all(jnp.broadcast_to(cotangent, (ch_devices, *cotangent.shape)), "ch")

    sent, pkv = pl.pallas_call(
        prepare_body,
        out_shape=(shape((seq_devices, 2, width, local_rows), bf16), shape(queries.shape, bf16)),
        cost_estimate=cost(3 << 20, 2 << 20),
    )(key_in, value_in, filter_raw)
    signals = jnp.transpose(to_all(sent, "seq"), (1, 2, 0, 3))

    conv, spectra = pl.pallas_call(
        conv_body,
        out_shape=(
            shape((width, seq_devices, local_rows), bf16),
            shape((2, width, half, 2 * LANES), f32),
        ),
        scratch_shapes=[pltpu.VMEM((2, width, half, 2 * LANES), f32)],
        cost_estimate=cost(1 << 31, 4 << 20),
    )(signals, *table)

    whole = lambda dims: pl.BlockSpec(dims, lambda i: (0,) * len(dims))
    mixed, grad_conv, g_sent = pl.pallas_call(
        mixed_body,
        grid=(ch_devices,),
        in_specs=[
            pl.BlockSpec((1, local_rows, local_width), lambda i: (i, 0, 0)),
            pl.BlockSpec((local_width, local_width), lambda i: (0, i)),
            whole(queries.shape),
        ],
        out_specs=(whole(queries.shape), whole(queries.shape), whole(message)),
        out_shape=(shape(queries.shape, f32), shape(queries.shape, bf16), shape(message, bf16)),
        cost_estimate=cost(1 << 31, 8 << 20),
    )(copies, out_weight, queries)

    both = jnp.stack([jnp.transpose(conv, (1, 0, 2)), g_sent], 1)
    both = to_all(both, "seq")

    partial, convolved = pl.pallas_call(
        gate_body,
        grid=(ch_devices,),
        in_specs=[
            whole(message),
            whole(queries.shape),
            whole(skip.shape),
            whole(queries.shape),
            pl.BlockSpec((local_width, local_width), lambda i: (0, i)),
        ],
        out_specs=(
            pl.BlockSpec((1, local_rows, local_width), lambda i: (i, 0, 0)),
            whole(queries.shape),
        ),
        out_shape=(
            shape((ch_devices, local_rows, local_width), bf16),
            shape(queries.shape, f32),
        ),
        scratch_shapes=[pltpu.VMEM(queries.shape, bf16)],
        cost_estimate=cost(1 << 31, 8 << 20),
    )(both[:, 0], pkv, skip, queries, out_weight)
    terms = to_all(partial, "ch")

    results = pl.pallas_call(
        back_body,
        out_shape=shape((2, width, seq_devices, local_rows), bf16),
        scratch_shapes=[pltpu.VMEM((2, width, half, 2 * LANES), f32)],
        cost_estimate=cost(1 << 31, 4 << 20),
    )(jnp.transpose(both[:, 1], (1, 0, 2)), spectra, *table)
    results = to_all(jnp.transpose(results, (2, 0, 1, 3)), "seq")

    grad_query = (mixed * convolved).astype(bf16)
    grad_key, grad_value, grad_filter = pl.pallas_call(
        finish_body,
        out_shape=(shape(queries.shape, bf16),) * 3,
        cost_estimate=cost(3 << 20, 2 << 20),
    )(results, grad_conv, skip, key_in, value_in)
    projected = jnp.sum(terms.astype(f32), axis=0).astype(bf16)
    return (projected, grad_query, grad_key, grad_value, grad_filter)


def solution(mesh):
    placed = (
        P("seq", "ch"),
        P("seq", "ch"),
        P("seq", "ch"),
        P("seq", "ch"),
        P("ch"),
        P("ch", None),
        P("seq", "ch"),
    )
    return jax.shard_map(
        on_device,
        mesh=mesh,
        in_specs=placed,
        out_specs=(P("seq", "ch"),) * 5,
        check_vma=False,
    )
```

time: 207 us -> 164 us (0.79); the launches traced: 204 us -> 163 us
  matrix products: 60.3 us -> 0 us
  Pallas kernels: 0 us -> 31.3 us
  waiting for transfers between devices: 72.4 us -> 49.8 us
  blocking collectives: 29.1 us -> 51.2 us
  starting transfers between devices: 24.9 us -> 16 us
  other arithmetic: 6.53 us -> 3.86 us
    dot_general x14 -> x0, matrix products: 60.3 us -> none  [the longest x8 43.3 us: contract(): return jnp.einsum(form, table, values, precision=precise)]
    pallas_call x0 -> x6, Pallas kernels: none -> 31.3 us  [the longest x1 7.87 us: on_device(): pl.pallas_call(mixed_body, grid=(ch_devices,), in_specs=[pl.BlockSpec((1,...]
    all_to_all x3, waiting for transfers between devices: 72.4 us -> 49.8 us  [to_all(): return lax.all_to_all(x, axis, split_axis=0, concat_axis=0, tiled=True)]
    all_to_all x1 -> x2, blocking collectives: 29.1 us -> 51.2 us  [to_all(): return lax.all_to_all(x, axis, split_axis=0, concat_axis=0, tiled=True)]
    all_to_all x3, starting transfers between devices: 24.9 us -> 16 us  [to_all(): return lax.all_to_all(x, axis, split_axis=0, concat_axis=0, tiled=True)]
    pallas_call x0 -> x2, local copies, waits for them, and re-layouts: none -> 3.24 us  [the longest x1 2.14 us: on_device(): pl.pallas_call(back_body, out_shape=shape((2, width, seq_devices, local_r...]
    convert_element_type x2 -> x0, local copies, waits for them, and re-layouts: 2.21 us -> none  [the longest x1 1.77 us: on_device(): grad_filter = results[2].astype(jnp.bfloat16)]
  transfers between devices with their start and end apart: 3 -> 3, of which waited for: 3 -> 3; matrix products, arithmetic and copies ran while one was open for 2% -> 2% of each run, Pallas kernels for 0% -> 9%
where the time goes in v1:
time: 164 us; the launch traced here: 163 us
  blocking collectives  51.2 us (31%)
  waiting for transfers between devices  49.8 us (30%)
  Pallas kernels  31.3 us (19%)
  starting transfers between devices  16 us (10%)
  local copies, waits for them, and re-layouts  10.5 us (6%)
  other arithmetic  3.86 us (2%)
    all_to_all x2, blocking collectives, to_all(): return lax.all_to_all(x, axis, split_axis=0, concat_axis=0, tiled=True)  51.2 us
    all_to_all x3, waiting for transfers between devices, to_all(): return lax.all_to_all(x, axis, split_axis=0, concat_axis=0, tiled=True)  49.8 us
    all_to_all x3, starting transfers between devices, to_all(): return lax.all_to_all(x, axis, split_axis=0, concat_axis=0, tiled=True)  16 us
    pallas_call x1, Pallas kernels, on_device(): pl.pallas_call(mixed_body, grid=(ch_devices,), in_specs=[pl.BlockSpec((1,...  7.87 us
    pallas_call x1, Pallas kernels, on_device(): pl.pallas_call(gate_body, grid=(ch_devices,), in_specs=[whole(message), w...  7.59 us
    pallas_call x1, Pallas kernels, on_device(): pl.pallas_call(back_body, out_shape=shape((2, width, seq_devices, local_r...  5.94 us
    pallas_call x1, Pallas kernels, on_device(): pl.pallas_call(conv_body, out_shape=(shape((width, seq_devices, local_row...  5.4 us
  transfers between devices with their start and end apart: 3, of which 3 were waited for; matrix products, arithmetic and copies ran while one was open for 2% of the time, Pallas kernels for 9%

profile of v1, /device:TPU:1, one launch (start us, length us, event | category | flops | bytes accessed | tf_op | source)
XLA Modules:
  0.0 163.4 jit_solution(16301654033789239868)
XLA Ops:
  0.6 2.1 %shard_map.155 = (bf16[32,2,16,256]{3,2,1,0:T(8,128)(2,1)}, bf16[256,512]{1,0:T(8,128)(2,1)}) custom-call(bf16[256,512]{1,0:T(8,128)(2,1)} %key_ref.3, bf16[256,512]{1,0:T(8,128)(2,1)} %value_ref.3, bf16[256,512]{1,0:T(8,128)(2,1)} %filter_ref.1), custom_call_target="tpu_custom_call" | custom-call | flops 3145728 | bytes 2097152 | tf_op jit(solution)/shard_map/pallas_call | solution.py:212
  2.7 30.4 %all_to_all.25 = bf16[32,2,16,256]{3,2,1,0:T(8,128)(2,1)S(1)} all-to-all(bf16[32,2,16,256]{3,2,1,0:T(8,128)(2,1)} %get-tuple-element.17), channel_id=1, replica_groups=mesh['seq'=32,'ch'=8] {'seq'}, dimensions={0} | all-to-all | bytes 1048576 | tf_op jit(solution)/shard_map/all_to_all | solution.py:195
  33.1 2.4 %broadcast_in_dim.3 = bf16[8,256,512]{2,1,0:T(8,128)(2,1)} broadcast(bf16[256,512]{1,0:T(8,128)(2,1)} %param.18), dimensions={1,2} | broadcast | bytes 2359296 | tf_op jit(solution)/shard_map/broadcast_in_dim | solution.py:210
  35.6 5.9 %all-to-all-start.1 = ((bf16[8,256,512]{2,1,0:T(8,128)(2,1)}), bf16[8,256,512]{2,1,0:T(8,128)(2,1)S(1)}, u32[]{:S(2)}, u32[]{:S(2)}) async-start(bf16[8,256,512]{2,1,0:T(8,128)(2,1)} %broadcast_in_dim.3), calls=%async_computation.1 | async-start | bytes 4194304 | tf_op jit(solution)/shard_map/all_to_all | solution.py:195
  41.4 1.1 copy.34
  42.5 5.4 %shard_map.156 = (bf16[16,32,256]{2,1,0:T(8,128)(2,1)}, f32[2,16,64,256]{3,2,1,0:T(8,128)}) custom-call(bf16[2,16,32,256]{3,2,1,0:T(8,128)(2,1)} %bitcast.23, bf16[256,64]{1,0:T(8,128)(2,1)} %constant.13.clone.first_ref, bf16[2,256,256]{2,1,0:T(8,128)(2,1)} %constant.14.clone.over_ref, bf16[2,256,256]{2,1,0:T(8,128)(2,1)} %constant.15.clone.under_ref, ...), custom_call_target="tpu_custom_call" | custom-call | flops 2147483648 | bytes 4194304 | tf_op jit(solution)/shard_map/pallas_call | solution.py:219
  47.9 1.1 copy.36
  49.0 18.6 %all-to-all-done.1.cot_ref = bf16[8,256,512]{2,1,0:T(8,128)(2,1)S(1)} async-done(((bf16[8,256,512]{2,1,0:T(8,128)(2,1)}), bf16[8,256,512]{2,1,0:T(8,128)(2,1)S(1)}, u32[]{:S(2)}, u32[]{:S(2)}) %all-to-all-start.1) | async-done | bytes 2097184 | tf_op jit(solution)/shard_map/all_to_all | solution.py:195
  67.6 0.0 copy-start.1
  67.6 1.3 copy-done.1
  69.0 7.9 %shard_map.157 = (f32[256,512]{1,0:T(8,128)}, bf16[256,512]{1,0:T(8,128)(2,1)}, bf16[32,16,256]{2,1,0:T(8,128)(2,1)}) custom-call(bf16[8,256,512]{2,1,0:T(8,128)(2,1)} %copy-done.1, bf16[512,4096]{1,0:T(8,128)(2,1)} %weight_ref.3, bf16[256,512]{1,0:T(8,128)(2,1)} %queries_ref.3), custom_call_target="tpu_custom_call" | custom-call | flops 2147483648 | bytes 8388608 | tf_op jit(solution)/shard_map/pallas_call | solution.py:230
  76.8 1.0 pad_maximum_fusion
  77.8 0.1 copy.23
  77.9 20.9 %all_to_all.26 = bf16[32,2,16,256]{3,2,1,0:T(8,128)(2,1)S(1)} all-to-all(bf16[32,2,16,256]{3,2,1,0:T(8,128)(2,1)S(1)} %copy.23), channel_id=1, replica_groups=mesh['seq'=32,'ch'=8] {'seq'}, dimensions={0} | all-to-all | bytes 1048576 | tf_op jit(solution)/shard_map/all_to_all | solution.py:195
  98.7 0.7 fusion
  99.5 0.8 copy.35
  100.3 5.9 %shard_map.159 = bf16[2,16,32,256]{3,2,1,0:T(8,128)(2,1)} custom-call(bf16[16,32,256]{2,1,0:T(8,128)(2,1)} %bitcast.24, f32[2,16,64,256]{3,2,1,0:T(8,128)} %get-tuple-element.24.spec_ref, bf16[256,64]{1,0:T(8,128)(2,1)} %constant.13.clone.first_ref, bf16[2,256,256]{2,1,0:T(8,128)(2,1)} %constant.14.clone.over_ref, ...), custom_call_target="tpu_custom_call" | custom-call | flops 2147483648 | bytes 4194304 | tf_op jit(solution)/shard_map/pallas_call | solution.py:269
  106.2 2.1 %copy.33 = bf16[2,16,32,256]{3,1,0,2:T(8,128)(2,1)} copy(bf16[2,16,32,256]{3,2,1,0:T(8,128)(2,1)} %shard_map.159) | data formatting | bytes 1048576 | tf_op jit(solution)/shard_map/pallas_call | solution.py:269
  108.3 4.9 %all-to-all-start.4 = ((bf16[32,2,16,256]{3,2,1,0:T(8,128)(2,1)}), bf16[32,2,16,256]{3,2,1,0:T(8,128)(2,1)S(1)}, u32[]{:S(2)}, u32[]{:S(2)}) async-start(bf16[32,2,16,256]{3,2,1,0:T(8,128)(2,1)} %bitcast.18), calls=%async_computation.4 | async-start | bytes 1048576 | tf_op jit(solution)/shard_map/all_to_all | solution.py:195
  113.3 7.6 %shard_map.158 = (bf16[8,256,512]{2,1,0:T(8,128)(2,1)}, f32[256,512]{1,0:T(8,128)}) custom-call(bf16[32,16,256]{2,1,0:T(8,128)(2,1)} %get-tuple-element.30.conv_ref, bf16[256,512]{1,0:T(8,128)(2,1)} %get-tuple-element.20.pkv_ref, f32[1,512]{1,0:T(1,128)} %bitcast.26, bf16[256,512]{1,0:T(8,128)(2,1)} %queries_ref.3, bf16[512,4096]{1,0:T(8,128)(2,1)} %weight_ref.3), custom_call_target="tpu_custom_call" | custom-call | flops 2147483648 | bytes 8388608 | tf_op jit(solution)/shard_map/pallas_call | solution.py:246
  120.9 9.3 %all-to-all-done.4.res_ref = bf16[32,2,16,256]{3,2,1,0:T(8,128)(2,1)S(1)} async-done(((bf16[32,2,16,256]{3,2,1,0:T(8,128)(2,1)}), bf16[32,2,16,256]{3,2,1,0:T(8,128)(2,1)S(1)}, u32[]{:S(2)}, u32[]{:S(2)}) %all-to-all-start.4) | async-done | bytes 524320 | tf_op jit(solution)/shard_map/all_to_all | solution.py:195
  130.1 0.0 copy-start
  130.1 0.0 copy-start.2
  130.1 0.8 copy-done
  130.9 5.2 %all-to-all-start.3 = ((bf16[8,256,512]{2,1,0:T(8,128)(2,1)}), bf16[8,256,512]{2,1,0:T(8,128)(2,1)S(1)}, u32[]{:S(2)}, u32[]{:S(2)}) async-start(bf16[8,256,512]{2,1,0:T(8,128)(2,1)} %get-tuple-element.21), calls=%async_computation.3 | async-start | bytes 4194304 | tf_op jit(solution)/shard_map/all_to_all | solution.py:195
  136.1 0.0 copy-done.2
  136.1 1.8 %multiply_convert_fusion = bf16[256,512]{1,0:T(8,128)(2,1)} fusion(f32[256,512]{1,0:T(8,128)S(1)} %copy-done.2, f32[256,512]{1,0:T(8,128)} %get-tuple-element.23), kind=kLoop, calls=%fused_computation.3 | loop fusion | flops 262144 | bytes 1310720 | tf_op jit(solution)/shard_map/convert_element_type | solution.py:277
  138.0 2.4 %shard_map.160 = (bf16[256,512]{1,0:T(8,128)(2,1)}, bf16[256,512]{1,0:T(8,128)(2,1)}, bf16[256,512]{1,0:T(8,128)(2,1)}) custom-call(bf16[32,2,16,256]{3,2,1,0:T(8,128)(2,1)} %copy-done, bf16[256,512]{1,0:T(8,128)(2,1)} %get-tuple-element.25.conv_ref, f32[1,512]{1,0:T(1,128)} %bitcast.27, bf16[256,512]{1,0:T(8,128)(2,1)} %key_ref.3, bf16[256,512]{1,0:T(8,128)(2,1)} %value_ref.3), custom_call_target="tpu_custom_call" | custom-call | flops 3145728 | bytes 2097152 | tf_op jit(solution)/shard_map/pallas_call | solution.py:278
  140.4 22.0 %all-to-all-done.3 = bf16[8,256,512]{2,1,0:T(8,128)(2,1)S(1)} async-done(((bf16[8,256,512]{2,1,0:T(8,128)(2,1)}), bf16[8,256,512]{2,1,0:T(8,128)(2,1)S(1)}, u32[]{:S(2)}, u32[]{:S(2)}) %all-to-all-start.3) | async-done | bytes 2097184 | tf_op jit(solution)/shard_map/all_to_all | solution.py:195
  162.3 1.0 reduce_sum.12
Async XLA Ops:
  35.6 32.1 %all-to-all-start.1 = ((bf16[8,256,512]{2,1,0:T(8,128)(2,1)}), bf16[8,256,512]{2,1,0:T(8,128)(2,1)S(1)}, u32[]{:S(2)}, u32[]{:S(2)}) async-start(bf16[8,256,512]{2,1,0:T(8,128)(2,1)} %broadcast_in_dim.3), calls=%async_computation.1 | async-start | bytes 4194304 | tf_op jit(solution)/shard_map/all_to_all | solution.py:195
  67.6 1.3 copy-start.1
  108.3 21.8 %all-to-all-start.4 = ((bf16[32,2,16,256]{3,2,1,0:T(8,128)(2,1)}), bf16[32,2,16,256]{3,2,1,0:T(8,128)(2,1)S(1)}, u32[]{:S(2)}, u32[]{:S(2)}) async-start(bf16[32,2,16,256]{3,2,1,0:T(8,128)(2,1)} %bitcast.18), calls=%async_computation.4 | async-start | bytes 1048576 | tf_op jit(solution)/shard_map/all_to_all | solution.py:195
  130.1 0.8 copy-start
  130.1 6.0 %copy-start.2 = (f32[256,512]{1,0:T(8,128)S(1)}, f32[256,512]{1,0:T(8,128)}, u32[]{:S(2)}) copy-start(f32[256,512]{1,0:T(8,128)} %get-tuple-element.22) | copy-start | bytes 1572868
  130.9 31.4 %all-to-all-start.3 = ((bf16[8,256,512]{2,1,0:T(8,128)(2,1)}), bf16[8,256,512]{2,1,0:T(8,128)(2,1)S(1)}, u32[]{:S(2)}, u32[]{:S(2)}) async-start(bf16[8,256,512]{2,1,0:T(8,128)(2,1)} %get-tuple-element.21), calls=%async_computation.3 | async-start | bytes 4194304 | tf_op jit(solution)/shard_map/all_to_all | solution.py:195
